TPU v7x, 32 devices: a whole 2x2x4 slice. The times are simulated.
32 devices in a mesh: ep: 4 (over y, core), fs: 8 (over z, x).
Axes of the slice: x: 2, y: 2, z: 4, core: 2. Of those that a mesh axis runs over, the one named last changes fastest.
Arguments:
- grads: bfloat16 [4, 4, 128, 14336], P('ep', None, 'fs'), may hold values from -64 to 64
- counts: int32 [4, 4], replicated, may hold values from 16 to 2047
- weight: bfloat16 [4, 128, 14336], P('ep', 'fs'), may hold values from -3 to 3
- mom: float32 [4, 128, 14336], P('ep', 'fs'), may hold values from -64 to 64
- second: float32 [4, 128, 14336], P('ep', 'fs'), may hold values from 0.1 to 10
- in_weight: float32 [6, 32], replicated, may hold values from -2.5 to 2.5
- in_bias: float32 [32], replicated, may hold values from -3 to 3
- out_weight: float32 [32, 2], replicated, may hold values from -1 to 1
- out_bias: float32 [2], replicated, may hold values from -3 to 3
Outputs:
- new_weight: bfloat16 [4, 128, 14336], P('ep')
- new_mom: float32 [4, 128, 14336], P('ep', 'fs')
- new_second: float32 [4, 128, 14336], P('ep', 'fs')
All inputs are finite; a program needn't handle non-finite values.
Results may differ from a plain program's by a relative error of at most 0.0019.
Values may be sent and summed in bfloat16 or wider, within the bound.
A program may use at most 64 MiB of HBM per device.

v0:
```python
import jax
import jax.numpy as jnp
from jax import lax
from jax.sharding import PartitionSpec as P

MOMENTUM_DECAY = 0.9
SECOND_DECAY = 0.99
NORM_EPS = 1e-06
ROOT_EPS = 1e-08
STEP_SCALE = 0.2
EXP_SCALE = 0.5


def learned_step(
    gradient,
    mom_next,
    second_next,
    weight,
    grad_norm,
    mom_norm,
    in_weight,
    in_bias,
    out_weight,
    out_bias,
):
    inv_root = lax.rsqrt(second_next + ROOT_EPS)
    features = jnp.stack(
        [
            gradient / grad_norm,
            mom_next / mom_norm,
            mom_next * inv_root,
            gradient * inv_root,
            weight.astype(jnp.float32),
            jnp.broadcast_to(jnp.log(mom_norm), gradient.shape),
        ]
    )
    hidden = jax.nn.relu(
        jnp.einsum("fh,fab->hab", in_weight, features, precision=lax.Precision.HIGHEST)
        + in_bias[:, None, None]
    )
    outputs = (
        jnp.einsum("hk,hab->kab", out_weight, hidden, precision=lax.Precision.HIGHEST)
        + out_bias[:, None, None]
    )
    update = STEP_SCALE * outputs[0] * jnp.exp(EXP_SCALE * outputs[1])
    return (weight.astype(jnp.float32) - update).astype(jnp.bfloat16)


def add_sources(arrived):
    return jnp.sum(arrived.astype(jnp.float32), axis=0)


def per_device(grads, counts, weight, mom, second, in_weight, in_bias, out_weight, out_bias):
    source = lax.axis_index("ep")
    counts_f = counts.astype(jnp.float32)
    totals = jnp.sum(counts_f, axis=0)
    share_row = lax.dynamic_index_in_dim(counts_f, source, 0, keepdims=False) / totals
    weighted = share_row[None, :, None, None] * grads.astype(jnp.float32)
    outgoing = weighted.astype(jnp.bfloat16)
    gradient = add_sources(lax.all_to_all(outgoing, "ep", split_axis=1, concat_axis=0, tiled=True))[
        0
    ]
    mom_here = mom[0]
    second_here = second[0]
    mom_next = MOMENTUM_DECAY * mom_here + (1.0 - MOMENTUM_DECAY) * gradient
    second_next = SECOND_DECAY * second_here + (1.0 - SECOND_DECAY) * gradient * gradient
    entries = gradient.shape[0] * gradient.shape[1] * lax.axis_size("fs")
    grad_sq, mom_sq = lax.psum((jnp.sum(gradient * gradient), jnp.sum(mom_next * mom_next)), "fs")
    grad_norm = jnp.sqrt(grad_sq / entries + NORM_EPS)
    mom_norm = jnp.sqrt(mom_sq / entries + NORM_EPS)
    width = gradient.shape[1]

    def block_step(items):
        grad_block, mom_block, second_block, weight_block = items
        return learned_step(
            grad_block,
            mom_block,
            second_block,
            weight_block,
            grad_norm,
            mom_norm,
            in_weight,
            in_bias,
            out_weight,
            out_bias,
        )

    blocks = lax.map(
        block_step,
        (
            gradient.reshape(-1, 2, width),
            mom_next.reshape(-1, 2, width),
            second_next.reshape(-1, 2, width),
            weight[0].reshape(-1, 2, width),
        ),
    )
    updated = blocks.reshape(gradient.shape)
    gathered = lax.all_gather(updated[None], "fs", axis=1, tiled=True)
    return (gathered, mom_next[None], second_next[None])


def solution(mesh):
    in_specs = (
        P("ep", None, "fs", None),
        P(),
        P("ep", "fs", None),
        P("ep", "fs", None),
        P("ep", "fs", None),
        P(),
        P(),
        P(),
        P(),
    )
    out_specs = (P("ep", None, None), P("ep", "fs", None), P("ep", "fs", None))
    return jax.shard_map(
        per_device, mesh=mesh, in_specs=in_specs, out_specs=out_specs, check_vma=False
    )
```

profile of v0, /device:TPU:0, one launch (start us, length us, event | category | flops | bytes accessed | tf_op | source)
XLA Modules:
  0.0 230.4 jit_solution(16413111683950979025)
XLA Ops:
  8.6 3.1 %multiply_convert_fusion = bf16[1,4,16,14336]{3,2,0,1:T(8,128)(2,1)} fusion(bf16[1,4,16,14336]{3,2,1,0:T(8,128)(2,1)} %param.11, f32[4]{0:T(128)S(1)} %bitcast_divide_fusion), kind=kLoop, calls=%fused_computation.22 | loop fusion | flops 2752512 | bytes 3670032 | tf_op jit(solution)/shard_map/convert_element_type | solution.py:59
  11.7 4.3 %all-to-all-start = ((bf16[1,4,16,14336]{3,2,0,1:T(8,128)(2,1)}), bf16[1,4,16,14336]{3,2,0,1:T(8,128)(2,1)S(1)}, u32[]{:S(2)}, u32[]{:S(2)}) async-start(bf16[1,4,16,14336]{3,2,0,1:T(8,128)(2,1)} %multiply_convert_fusion), calls=%async_computation | async-start | bytes 3670016 | tf_op jit(solution)/shard_map/all_to_all | solution.py:60
  16.3 22.5 %all-to-all-done = bf16[1,4,16,14336]{3,2,0,1:T(8,128)(2,1)S(1)} async-done(((bf16[1,4,16,14336]{3,2,0,1:T(8,128)(2,1)}), bf16[1,4,16,14336]{3,2,0,1:T(8,128)(2,1)S(1)}, u32[]{:S(2)}, u32[]{:S(2)}) %all-to-all-start) | async-done | bytes 1835040 | tf_op jit(solution)/shard_map/all_to_all | solution.py:60
  42.6 23.1 %all-reduce = (f32[]{:T(128)}, f32[]{:T(128)}) all-reduce(f32[]{:T(128)} %get-tuple-element.159, f32[]{:T(128)} %get-tuple-element.158), channel_id=1, replica_groups=mesh['ep'=4,'fs'=8] {'fs'}, use_global_device_ids=true, to_apply=%region_3.4 | all-reduce | flops 2 | bytes 16 | tf_op jit(solution)/shard_map/psum | solution.py:68
  66.5 3.0 %fusion.10 = (f32[1,16,14336]{2,1,0:T(8,128)}, f32[1,16,14336]{2,1,0:T(8,128)S(1)}, f32[1,16,14336]{2,1,0:T(8,128)}, f32[1,16,14336]{2,1,0:T(8,128)S(1)}) fusion(f32[16,14336]{1,0:T(8,128)S(1)} %convert_reduce_fusion, f32[1,16,14336]{2,1,0:T(8,128)} %param.15, f32[1,16,14336]{2,1,0:T(8,128)} %param.14), kind=kLoop, calls=%fused_computation.26 | loop fusion | flops 1605632 | bytes 6422528 | tf_op jit(solution)/shard_map/add | solution.py:66
  72.2 4.1 %fusion.9 = (f32[8,2,14336]{2,0,1:T(8,128)S(1)}, f32[8,2,14336]{2,0,1:T(8,128)}, f32[8,2,14336]{2,0,1:T(8,128)}) fusion(f32[8,2,14336]{2,1,0:T(2,128)S(1)} %mul.131, f32[8,2,14336]{2,1,0:T(2,128)S(1)} %copy-done, f32[8,2,14336]{2,1,0:T(2,128)} %mul.122), kind=kLoop, calls=%fused_computation.25 | loop fusion | flops 1146880 | bytes 5505024 | tf_op jit(solution)/shard_map/add | solution.py:66
  76.3 78.5 %while.11 = (s32[]{:T(128)}, bf16[8,2,14336]{2,1,0:T(2,128)(2,1)}, bf16[8,2,14336]{2,1,0:T(2,128)(2,1)S(1)}, f32[8,2,14336]{2,0,1:T(8,128)}, f32[]{:T(128)}, /*i...) while((s32[]{:T(128)}, bf16[8,2,14336]{2,1,0:T(2,128)(2,1)}, ...), condition=%wide.region_7.8_spmd, body=%wide.region_6.7_spmd.sunk | while | flops 90316800 | bytes 18638680 | solution.py:88
  76.3 2.2 dynamic-slice_multiply_fusion.3
  79.9 3.2 %fusion.27 = f32[32,2,14336]{2,0,1:T(8,128)S(1)} fusion(f32[6,2,14336]{2,0,1:T(8,128)S(1)} %stack.4, f32[32]{0:T(128)S(1)} %get-tuple-element.324, f32[6,32]{1,0:T(8,128)S(1)} %get-tuple-element.323), kind=kOutput, calls=%fused_computation.2.clone.1 | convolution fusion | flops 67895296 | bytes 4359040 | tf_op jit(solution)/shard_map/while/body/eval_jaxpr/fh,fab->hab/dot_general | solution.py:38
  86.2 2.2 dynamic-slice_multiply_fusion.3
  89.7 3.2 %fusion.27 = f32[32,2,14336]{2,0,1:T(8,128)S(1)} fusion(f32[6,2,14336]{2,0,1:T(8,128)S(1)} %stack.4, f32[32]{0:T(128)S(1)} %get-tuple-element.324, f32[6,32]{1,0:T(8,128)S(1)} %get-tuple-element.323), kind=kOutput, calls=%fused_computation.2.clone.1 | convolution fusion | flops 67895296 | bytes 4359040 | tf_op jit(solution)/shard_map/while/body/eval_jaxpr/fh,fab->hab/dot_general | solution.py:38
  96.0 2.2 dynamic-slice_multiply_fusion.3
  99.5 3.2 %fusion.27 = f32[32,2,14336]{2,0,1:T(8,128)S(1)} fusion(f32[6,2,14336]{2,0,1:T(8,128)S(1)} %stack.4, f32[32]{0:T(128)S(1)} %get-tuple-element.324, f32[6,32]{1,0:T(8,128)S(1)} %get-tuple-element.323), kind=kOutput, calls=%fused_computation.2.clone.1 | convolution fusion | flops 67895296 | bytes 4359040 | tf_op jit(solution)/shard_map/while/body/eval_jaxpr/fh,fab->hab/dot_general | solution.py:38
  105.8 2.2 dynamic-slice_multiply_fusion.3
  109.3 3.2 %fusion.27 = f32[32,2,14336]{2,0,1:T(8,128)S(1)} fusion(f32[6,2,14336]{2,0,1:T(8,128)S(1)} %stack.4, f32[32]{0:T(128)S(1)} %get-tuple-element.324, f32[6,32]{1,0:T(8,128)S(1)} %get-tuple-element.323), kind=kOutput, calls=%fused_computation.2.clone.1 | convolution fusion | flops 67895296 | bytes 4359040 | tf_op jit(solution)/shard_map/while/body/eval_jaxpr/fh,fab->hab/dot_general | solution.py:38
  119.1 3.2 %fusion.27 = f32[32,2,14336]{2,0,1:T(8,128)S(1)} fusion(f32[6,2,14336]{2,0,1:T(8,128)S(1)} %stack.4, f32[32]{0:T(128)S(1)} %get-tuple-element.324, f32[6,32]{1,0:T(8,128)S(1)} %get-tuple-element.323), kind=kOutput, calls=%fused_computation.2.clone.1 | convolution fusion | flops 67895296 | bytes 4359040 | tf_op jit(solution)/shard_map/while/body/eval_jaxpr/fh,fab->hab/dot_general | solution.py:38
  125.4 2.2 dynamic-slice_multiply_fusion.3
  128.9 3.2 %fusion.27 = f32[32,2,14336]{2,0,1:T(8,128)S(1)} fusion(f32[6,2,14336]{2,0,1:T(8,128)S(1)} %stack.4, f32[32]{0:T(128)S(1)} %get-tuple-element.324, f32[6,32]{1,0:T(8,128)S(1)} %get-tuple-element.323), kind=kOutput, calls=%fused_computation.2.clone.1 | convolution fusion | flops 67895296 | bytes 4359040 | tf_op jit(solution)/shard_map/while/body/eval_jaxpr/fh,fab->hab/dot_general | solution.py:38
  135.2 2.2 dynamic-slice_multiply_fusion.3
  138.7 3.2 %fusion.27 = f32[32,2,14336]{2,0,1:T(8,128)S(1)} fusion(f32[6,2,14336]{2,0,1:T(8,128)S(1)} %stack.4, f32[32]{0:T(128)S(1)} %get-tuple-element.324, f32[6,32]{1,0:T(8,128)S(1)} %get-tuple-element.323), kind=kOutput, calls=%fused_computation.2.clone.1 | convolution fusion | flops 67895296 | bytes 4359040 | tf_op jit(solution)/shard_map/while/body/eval_jaxpr/fh,fab->hab/dot_general | solution.py:38
  145.0 2.2 dynamic-slice_multiply_fusion.3
  148.5 3.2 %fusion.27 = f32[32,2,14336]{2,0,1:T(8,128)S(1)} fusion(f32[6,2,14336]{2,0,1:T(8,128)S(1)} %stack.4, f32[32]{0:T(128)S(1)} %get-tuple-element.324, f32[6,32]{1,0:T(8,128)S(1)} %get-tuple-element.323), kind=kOutput, calls=%fused_computation.2.clone.1 | convolution fusion | flops 67895296 | bytes 4359040 | tf_op jit(solution)/shard_map/while/body/eval_jaxpr/fh,fab->hab/dot_general | solution.py:38
  156.8 62.5 %all-gather.2.cloned.1.call-done = bf16[1,128,14336]{2,1,0:T(8,128)(2,1)} async-done(((bf16[1,16,14336]{2,1,0:T(8,128)(2,1)}), bf16[1,128,14336]{2,1,0:T(8,128)(2,1)}) %all-gather.2.cloned.1.call-update) | async-done | bytes 3670032 | tf_op jit(solution)/shard_map/all_gather | solution.py:98
  219.3 4.2 %copy.64 = bf16[1,128,14336]{2,1,0:T(8,128)(2,1)} copy(bf16[1,128,14336]{2,1,0:T(8,128)(2,1)} %all-gather.2.cloned.1.call-done) | data formatting | bytes 7340032
  (114 shorter events, 46.7 us)
Async XLA Ops:
  8.6 7.4 %copy-start.3 = (bf16[1,16,14336]{2,1,0:T(8,128)(2,1)S(1)}, bf16[1,16,14336]{2,1,0:T(8,128)(2,1)}, u32[]{:S(2)}) copy-start(bf16[1,16,14336]{2,1,0:T(8,128)(2,1)} %param.13) | copy-start | bytes 1376260
  11.7 27.1 %all-to-all-start = ((bf16[1,4,16,14336]{3,2,0,1:T(8,128)(2,1)}), bf16[1,4,16,14336]{3,2,0,1:T(8,128)(2,1)S(1)}, u32[]{:S(2)}, u32[]{:S(2)}) async-start(bf16[1,4,16,14336]{3,2,0,1:T(8,128)(2,1)} %multiply_convert_fusion), calls=%async_computation | async-start | bytes 3670016 | tf_op jit(solution)/shard_map/all_to_all | solution.py:60
  16.0 203.3 %all-gather.2.cloned.1.call-start = ((), (), s32[]{:S(2)}) async-start(), calls=%async_computation.1 | async-start | bytes 4128768 | tf_op jit(solution)/shard_map/all_gather | solution.py:98
  69.4 2.8 %copy-start = (f32[8,2,14336]{2,1,0:T(2,128)S(1)}, f32[8,2,14336]{2,1,0:T(2,128)}, u32[]{:S(2)}) copy-start(f32[8,2,14336]{2,1,0:T(2,128)} %reshape_squeeze.7) | copy-start | bytes 2752516
  70.9 5.4 %copy-start.4 = (f32[6,32]{1,0:T(8,128)S(1)}, f32[6,32]{1,0:T(8,128)}, u32[]{:S(2)}) copy-start(f32[6,32]{1,0:T(8,128)} %param.16) | copy-start | bytes 2308
  70.9 5.4 %copy-start.5 = (f32[32,2]{0,1:T(2,128)S(1)}, f32[32,2]{0,1:T(2,128)}, u32[]{:S(2)}) copy-start(f32[32,2]{0,1:T(2,128)} %param.18) | copy-start | bytes 772
  70.9 5.4 %copy-start.6 = (f32[32]{0:T(128)S(1)}, f32[32]{0:T(128)}, u32[]{:S(2)}) copy-start(f32[32]{0:T(128)} %param.17) | copy-start | bytes 388
  70.9 5.4 %copy-start.7 = (f32[2]{0:T(128)S(1)}, f32[2]{0:T(128)}, u32[]{:S(2)}) copy-start(f32[2]{0:T(128)} %param.19) | copy-start | bytes 28
  76.3 2.2 copy-start.1
  83.1 3.1 %copy-start.2 = (f32[8,2,14336]{2,0,1:T(8,128)S(1)}, f32[8,2,14336]{2,0,1:T(8,128)}, u32[]{:S(2)}) copy-start(f32[8,2,14336]{2,0,1:T(8,128)} %copy-done.1) | copy-start | bytes 2752516 | tf_op jit(solution)/shard_map/while
  86.2 2.2 copy-start.1
  92.9 3.1 %copy-start.2 = (f32[8,2,14336]{2,0,1:T(8,128)S(1)}, f32[8,2,14336]{2,0,1:T(8,128)}, u32[]{:S(2)}) copy-start(f32[8,2,14336]{2,0,1:T(8,128)} %copy-done.1) | copy-start | bytes 2752516 | tf_op jit(solution)/shard_map/while
  96.0 2.2 copy-start.1
  102.7 3.1 %copy-start.2 = (f32[8,2,14336]{2,0,1:T(8,128)S(1)}, f32[8,2,14336]{2,0,1:T(8,128)}, u32[]{:S(2)}) copy-start(f32[8,2,14336]{2,0,1:T(8,128)} %copy-done.1) | copy-start | bytes 2752516 | tf_op jit(solution)/shard_map/while
  105.8 2.2 copy-start.1
  112.5 3.1 %copy-start.2 = (f32[8,2,14336]{2,0,1:T(8,128)S(1)}, f32[8,2,14336]{2,0,1:T(8,128)}, u32[]{:S(2)}) copy-start(f32[8,2,14336]{2,0,1:T(8,128)} %copy-done.1) | copy-start | bytes 2752516 | tf_op jit(solution)/shard_map/while
  115.6 2.2 copy-start.1
  122.3 3.1 %copy-start.2 = (f32[8,2,14336]{2,0,1:T(8,128)S(1)}, f32[8,2,14336]{2,0,1:T(8,128)}, u32[]{:S(2)}) copy-start(f32[8,2,14336]{2,0,1:T(8,128)} %copy-done.1) | copy-start | bytes 2752516 | tf_op jit(solution)/shard_map/while
  125.4 2.2 copy-start.1
  132.1 3.1 %copy-start.2 = (f32[8,2,14336]{2,0,1:T(8,128)S(1)}, f32[8,2,14336]{2,0,1:T(8,128)}, u32[]{:S(2)}) copy-start(f32[8,2,14336]{2,0,1:T(8,128)} %copy-done.1) | copy-start | bytes 2752516 | tf_op jit(solution)/shard_map/while
  135.2 2.2 copy-start.1
  141.9 3.1 %copy-start.2 = (f32[8,2,14336]{2,0,1:T(8,128)S(1)}, f32[8,2,14336]{2,0,1:T(8,128)}, u32[]{:S(2)}) copy-start(f32[8,2,14336]{2,0,1:T(8,128)} %copy-done.1) | copy-start | bytes 2752516 | tf_op jit(solution)/shard_map/while
  145.0 2.2 copy-start.1
  151.8 3.1 %copy-start.2 = (f32[8,2,14336]{2,0,1:T(8,128)S(1)}, f32[8,2,14336]{2,0,1:T(8,128)}, u32[]{:S(2)}) copy-start(f32[8,2,14336]{2,0,1:T(8,128)} %copy-done.1) | copy-start | bytes 2752516 | tf_op jit(solution)/shard_map/while
Sparse Core Ops, SparseCore 0:
  156.9 62.3 all-gather.1
where the time goes:
time: 231 us; the launch traced here: 230 us
  waiting for transfers between devices  85.1 us (37%)
  matrix products  42 us (18%)
  other arithmetic  34.4 us (15%)
  local copies, waits for them, and re-layouts  25.4 us (11%)
  blocking collectives  23.1 us (10%)
  between operations  15.5 us (7%)
  starting transfers between devices  4.27 us (2%)
    all_gather x1, waiting for transfers between devices, per_device(): gathered = lax.all_gather(updated[None], 'fs', axis=1, tiled=True)  62.5 us
    dot_general x8, matrix products, learned_step(): jnp.einsum('fh,fab->hab', in_weight, features, precision=lax.Precision.HI...  25.6 us
    psum x1, blocking collectives, per_device(): lax.psum((jnp.sum(gradient * gradient), jnp.sum(mom_next * mom_next)), 'fs')  23.1 us
    all_to_all x1, waiting for transfers between devices, per_device(): lax.all_to_all(outgoing, 'ep', split_axis=1, concat_axis=0, tiled=True)  22.5 us
    mul x8, other arithmetic, learned_step(): gradient * inv_root  17.3 us
    dot_general x8, matrix products, learned_step(): jnp.einsum('hk,hab->kab', out_weight, hidden, precision=lax.Precision.HIG...  16.4 us
    another operation x8, local copies, waits for them, and re-layouts, learned_step(): jnp.stack([gradient / grad_norm, mom_next / mom_norm, mom_next * inv_root...  8.98 us
    add x2, other arithmetic, per_device(): SECOND_DECAY * second_here + (1.0 - SECOND_DECAY) * gradient * gradient  7.04 us
  transfers between devices with their start and end apart: 2, of which 2 were waited for; matrix products, arithmetic and copies ran while one was open for 0% of the time, Pallas kernels for 0%

commit v1 on v0

v1 whole, which is shorter than its diff:
```python
import functools

import jax
import jax.numpy as jnp
from jax import lax
from jax.experimental import pallas as pl
from jax.experimental.pallas import tpu as pltpu
from jax.sharding import PartitionSpec as P

MOMENTUM_DECAY = 0.9
SECOND_DECAY = 0.99
NORM_EPS = 1e-06
ROOT_EPS = 1e-08
STEP_SCALE = 0.2
EXP_SCALE = 0.5
LANES = 128
MOST_CHUNKS = 8


def largest_divisor(number, most):
    return max(d for d in range(1, most + 1) if number % d == 0)


def tile_width(columns, most):
    return LANES * largest_divisor(columns // LANES, most // LANES)


def remote(src, dst, send_sem, recv_sem, axis, peer):
    return pltpu.make_async_remote_copy(
        src_ref=src,
        dst_ref=dst,
        send_sem=send_sem,
        recv_sem=recv_sem,
        device_id={axis: peer},
        device_id_type=pl.DeviceIdType.MESH,
    )


def kernel(
    groups,
    depth,
    across,
    chunks,
    counts,
    in_weight,
    in_bias,
    out_weight,
    out_bias,
    grads,
    weight,
    mom,
    second,
    gathered,
    mom_out,
    second_out,
    outgoing,
    arrived,
    gradient,
    sums,
    bias,
    grad_send,
    grad_recv,
    sum_send,
    sum_recv,
    row_send,
    row_recv,
):
    shards = depth * across
    rows, columns = mom.shape[1], mom.shape[2]
    units = in_bias.shape[0]
    me_group = lax.axis_index("ep")
    me = lax.axis_index("fs")
    z = me // across
    x = me % across

    barrier = pltpu.get_barrier_semaphore()
    for step in range(1, groups):
        pl.semaphore_signal(
            barrier,
            inc=1,
            device_id={"ep": (me_group + step) % groups},
            device_id_type=pl.DeviceIdType.MESH,
        )
    for step in range(1, shards):
        pl.semaphore_signal(
            barrier,
            inc=1,
            device_id={"fs": (me + step) % shards},
            device_id_type=pl.DeviceIdType.MESH,
        )
    pl.semaphore_wait(barrier, groups - 1 + shards - 1)

    wide = tile_width(columns, 1024)

    def share_of(expert):
        total = counts[0, expert]
        for s in range(1, groups):
            total = total + counts[s, expert]
        mine = jnp.full((1, LANES), counts[me_group, expert].astype(jnp.float32))
        return (mine / jnp.full((1, LANES), total.astype(jnp.float32)))[:, :1]

    sends = []
    order = sorted(range(1, groups), key=lambda step: abs(2 * step - groups))
    for step in order:
        peer = (me_group + step) % groups
        share = share_of(peer)

        def weigh(i, carry, peer=peer, share=share, step=step):
            cols = pl.ds(pl.multiple_of(i * wide, wide), wide)
            value = share * grads[0, peer, :, cols].astype(jnp.float32)
            outgoing[step - 1, :, cols] = value.astype(jnp.bfloat16)
            return carry

        lax.fori_loop(0, columns // wide, weigh, 0)
        copy = remote(
            outgoing.at[step - 1],
            arrived.at[step - 1],
            grad_send.at[step - 1],
            grad_recv.at[step - 1],
            "ep",
            peer,
        )
        copy.start()
        sends.append(copy)
    for copy in sends:
        copy.wait_recv()

    share = share_of(me_group)
    narrow = tile_width(columns, 512)

    def moments(i, carry):
        grad_acc, mom_acc = carry
        cols = pl.ds(pl.multiple_of(i * narrow, narrow), narrow)
        own = (share * grads[0, me_group, :, cols].astype(jnp.float32)).astype(jnp.bfloat16)
        total = own.astype(jnp.float32)
        for s in range(groups - 1):
            total = total + arrived[s, :, cols].astype(jnp.float32)
        mom_next = MOMENTUM_DECAY * mom[0, :, cols] + (1.0 - MOMENTUM_DECAY) * total
        gradient[:, cols] = total
        mom_out[0, :, cols] = mom_next
        second_out[0, :, cols] = (
            SECOND_DECAY * second[0, :, cols] + (1.0 - SECOND_DECAY) * total * total
        )
        return grad_acc + total * total, mom_acc + mom_next * mom_next

    zero = jnp.zeros((rows, narrow), jnp.float32)
    grad_acc, mom_acc = lax.fori_loop(0, columns // narrow, moments, (zero, zero))

    def to_lanes(acc):
        acc = jnp.sum(acc, axis=0, keepdims=True)
        return sum(acc[:, j : j + LANES] for j in range(0, narrow, LANES))

    sums[me, 0:1, :] = to_lanes(grad_acc)
    sums[me, 1:2, :] = to_lanes(mom_acc)
    sum_sends = []
    for step in range(1, shards):
        copy = remote(
            sums.at[me],
            sums.at[me],
            sum_send.at[step - 1],
            sum_recv.at[me],
            "fs",
            (me + step) % shards,
        )
        copy.start()
        sum_sends.append(copy)
    for step in range(1, shards):
        source = (me + step) % shards
        remote(
            sums.at[source],
            sums.at[source],
            sum_send.at[step - 1],
            sum_recv.at[source],
            "fs",
            source,
        ).wait_recv()

    entries = rows * columns * shards
    totals = sums[0]
    for s in range(1, shards):
        totals = totals + sums[s]
    mean = jnp.broadcast_to(jnp.sum(totals, axis=1, keepdims=True) / entries, (2, LANES)) + NORM_EPS
    inverse = lax.rsqrt(mean)
    inv_grad = inverse[0:1, :1]
    inv_mom = inverse[1:2, :1]
    log_mom = jnp.max(0.5 * jnp.log(mean[1:2, :]))
    for h in range(units):
        bias[h] = in_bias[h] + in_weight[5, h] * log_mom

    width = columns // chunks
    tile = tile_width(width, 256)

    def learned_step(cols):
        grad = gradient[:, cols]
        mom_next = mom_out[0, :, cols]
        old = weight[0, :, cols].astype(jnp.float32)
        inv_root = lax.rsqrt(second_out[0, :, cols] + ROOT_EPS)
        features = (
            grad * inv_grad,
            mom_next * inv_mom,
            mom_next * inv_root,
            grad * inv_root,
            old,
        )
        direction = jnp.full(grad.shape, out_bias[0])
        magnitude = jnp.full(grad.shape, out_bias[1])
        for h in range(units):
            hidden = features[0] * in_weight[0, h] + bias[h]
            for f in range(1, len(features)):
                hidden = hidden + features[f] * in_weight[f, h]
            hidden = jnp.maximum(hidden, 0.0)
            direction = direction + hidden * out_weight[h, 0]
            magnitude = magnitude + hidden * out_weight[h, 1]
        update = STEP_SCALE * direction * jnp.exp(EXP_SCALE * magnitude)
        return (old - update).astype(jnp.bfloat16)

    def rows_of(source):
        return pl.ds(pl.multiple_of(source * rows, rows), rows)

    ways = (
        (0, across, z < depth - 1),
        (1, -across, z > 0),
        (2, 1, x < across - 1),
        (3, -1, x > 0),
    )

    def block(source, k, full=False):
        if full:
            return gathered.at[0, rows_of(source), :]
        return gathered.at[0, rows_of(source), pl.ds(pl.multiple_of(k * width, width), width)]

    def send(source, k, which):
        for number, offset, possible in ways:
            if number in which:

                @pl.when(possible)
                def _(number=number, offset=offset):
                    piece = block(source, k)
                    remote(
                        piece,
                        piece,
                        row_send.at[number, source],
                        row_recv.at[source, k],
                        "fs",
                        me + offset,
                    ).start()

    def await_block(source, k):
        piece = block(source, k)
        remote(
            piece, piece, row_send.at[0, source], row_recv.at[source, k], "fs", source
        ).wait_recv()

    def turn(t, carry):
        @pl.when(t < chunks)
        def _():
            def one(i, inner):
                cols = pl.ds(pl.multiple_of(t * width + i * tile, tile), tile)
                gathered[0, rows_of(me), cols] = learned_step(cols)
                return inner

            lax.fori_loop(0, width // tile, one, 0)
            send(me, t, (0, 1, 2, 3))

        for d in range(1, depth):
            live = jnp.logical_and(t >= d, t - d < chunks)

            @pl.when(jnp.logical_and(live, z >= d))
            def _(d=d):
                source = me - d * across
                await_block(source, t - d)
                send(source, t - d, (0, 2, 3))

            @pl.when(jnp.logical_and(live, z + d < depth))
            def _(d=d):
                source = me + d * across
                await_block(source, t - d)
                send(source, t - d, (1, 2, 3))

        for e in range(1, across):
            late = depth - 1 + e
            live = jnp.logical_and(t >= late, t - late < chunks)
            for level in range(depth):

                @pl.when(jnp.logical_and(live, x >= e))
                def _(e=e, late=late, level=level):
                    source = level * across + x - e
                    await_block(source, t - late)
                    send(source, t - late, (2,))

                @pl.when(jnp.logical_and(live, x + e < across))
                def _(e=e, late=late, level=level):
                    source = level * across + x + e
                    await_block(source, t - late)
                    send(source, t - late, (3,))

        return carry

    lax.fori_loop(0, chunks + depth - 1 + across - 1, turn, 0)

    for copy in sends:
        copy.wait_send()
    for copy in sum_sends:
        copy.wait_send()
    for number, _, possible in ways:
        for source in range(shards):
            level, place = source // across, source % across
            used = (
                jnp.logical_and(place == x, level <= z),
                jnp.logical_and(place == x, level >= z),
                place <= x,
                place >= x,
            )[number]

            @pl.when(jnp.logical_and(possible, used))
            def _(number=number, source=source):
                piece = block(source, 0, full=True)
                remote(
                    piece,
                    piece,
                    row_send.at[number, source],
                    row_recv.at[source, 0],
                    "fs",
                    (me + 1) % shards,
                ).wait_send()


def per_device(
    groups, shards, grads, counts, weight, mom, second, in_weight, in_bias, out_weight, out_bias
):
    rows, columns = mom.shape[1], mom.shape[2]
    across = max(d for d in range(1, shards + 1) if shards % d == 0 and d * d <= shards)
    depth = shards // across
    chunks = largest_divisor(columns // LANES, MOST_CHUNKS)
    smem = pl.BlockSpec(memory_space=pltpu.SMEM)
    vmem = pl.BlockSpec(memory_space=pltpu.VMEM)
    return pl.pallas_call(
        functools.partial(kernel, groups, depth, across, chunks),
        out_shape=(
            jax.ShapeDtypeStruct((1, rows * shards, columns), jnp.bfloat16),
            jax.ShapeDtypeStruct(mom.shape, jnp.float32),
            jax.ShapeDtypeStruct(second.shape, jnp.float32),
        ),
        in_specs=[smem] * 5 + [vmem] * 4,
        out_specs=(vmem, vmem, vmem),
        scratch_shapes=[
            pltpu.VMEM((groups - 1, rows, columns), jnp.bfloat16),
            pltpu.VMEM((groups - 1, rows, columns), jnp.bfloat16),
            pltpu.VMEM((rows, columns), jnp.float32),
            pltpu.VMEM((shards, 2, LANES), jnp.float32),
            pltpu.SMEM((in_bias.shape[0],), jnp.float32),
            pltpu.SemaphoreType.DMA((groups - 1,)),
            pltpu.SemaphoreType.DMA((groups - 1,)),
            pltpu.SemaphoreType.DMA((shards - 1,)),
            pltpu.SemaphoreType.DMA((shards,)),
            pltpu.SemaphoreType.DMA((4, shards)),
            pltpu.SemaphoreType.DMA((shards, chunks)),
        ],
        compiler_params=pltpu.CompilerParams(
            collective_id=0, has_side_effects=True, vmem_limit_bytes=48 * 1024 * 1024
        ),
        name="learned_update",
    )(counts, in_weight, in_bias, out_weight, out_bias, grads, weight, mom, second)


def solution(mesh):
    in_specs = (
        P("ep", None, "fs", None),
        P(),
        P("ep", "fs", None),
        P("ep", "fs", None),
        P("ep", "fs", None),
        P(),
        P(),
        P(),
        P(),
    )
    out_specs = (P("ep", None, None), P("ep", "fs", None), P("ep", "fs", None))
    body = functools.partial(per_device, mesh.shape["ep"], mesh.shape["fs"])
    return jax.shard_map(
        body, mesh=mesh, in_specs=in_specs, out_specs=out_specs, check_vma=False
    )
```

time: 231 us -> 95 us (0.41)
  waiting for transfers between devices: 85.1 us -> 0 us
  Pallas kernels: 0 us -> 79.6 us
  matrix products: 42 us -> 0 us
  other arithmetic: 34.4 us -> 0 us
  blocking collectives: 23.1 us -> 0 us
  between operations: 15.5 us -> 0.65 us
  local copies, waits for them, and re-layouts: 25.4 us -> 14.4 us
  starting transfers between devices: 4.27 us -> 0 us
    pallas_call x0 -> x1, Pallas kernels: none -> 79.6 us  [per_device(): pl.pallas_call(functools.partial(kernel, groups, depth, across, chunks),...]
    all_gather x1 -> x0, waiting for transfers between devices: 62.5 us -> none  [per_device(): gathered = lax.all_gather(updated[None], 'fs', axis=1, tiled=True)]
    dot_general x16 -> x0, matrix products: 42 us -> none  [the longest x8 25.6 us: learned_step(): jnp.einsum('fh,fab->hab', in_weight, features, precision=lax.Precision.HI...]
    psum x1 -> x0, blocking collectives: 23.1 us -> none  [per_device(): lax.psum((jnp.sum(gradient * gradient), jnp.sum(mom_next * mom_next)), 'fs')]
    all_to_all x1 -> x0, waiting for transfers between devices: 22.5 us -> none  [per_device(): lax.all_to_all(outgoing, 'ep', split_axis=1, concat_axis=0, tiled=True)]
    mul x8 -> x0, other arithmetic: 17.3 us -> none  [learned_step(): gradient * inv_root]
    another operation x11 -> x0, local copies, waits for them, and re-layouts: 12.7 us -> none  [the longest x8 8.98 us: learned_step(): jnp.stack([gradient / grad_norm, mom_next / mom_norm, mom_next * inv_root...]
    unnamed x13 -> x20, local copies, waits for them, and re-layouts: 4.22 us -> 14.4 us
  transfers between devices with their start and end apart: 2 -> 0, of which waited for: 2 -> 0; matrix products, arithmetic and copies ran while one was open for 0% -> 0% of each run, Pallas kernels for 0% -> 0%
where the time goes in v1:
time: 95 us; the launch traced here: 94.6 us
  Pallas kernels  79.6 us (84%)
  local copies, waits for them, and re-layouts  14.4 us (15%)
    pallas_call x1, Pallas kernels, per_device(): pl.pallas_call(functools.partial(kernel, groups, depth, across, chunks),...  79.6 us
    unnamed x20, local copies, waits for them, and re-layouts  14.4 us

profile of v1, /device:TPU:0, one launch (start us, length us, event | category | flops | bytes accessed | tf_op | source)
XLA Modules:
  0.0 94.6 jit_solution(9183938754496135845)
XLA Ops:
  0.6 0.8 copy.12.out_weight
  1.4 0.0 copy-start
  1.4 1.5 %copy-done = bf16[1,4,16,14336]{3,2,1,0:T(8,128)(2,1)S(1)} copy-done((bf16[1,4,16,14336]{3,2,1,0:T(8,128)(2,1)S(1)}, bf16[1,4,16,14336]{3,2,1,0:T(8,128)(2,1)}, u32[]{:S(2)}) %copy-start) | copy-done | bytes 1835032
  2.9 0.0 copy-start.1
  2.9 1.2 %copy-done.1 = f32[1,16,14336]{2,1,0:T(8,128)S(1)} copy-done((f32[1,16,14336]{2,1,0:T(8,128)S(1)}, f32[1,16,14336]{2,1,0:T(8,128)}, u32[]{:S(2)}) %copy-start.1) | copy-done | bytes 917528
  4.1 0.0 copy-start.2
  4.1 1.2 %copy-done.2 = f32[1,16,14336]{2,1,0:T(8,128)S(1)} copy-done((f32[1,16,14336]{2,1,0:T(8,128)S(1)}, f32[1,16,14336]{2,1,0:T(8,128)}, u32[]{:S(2)}) %copy-start.2) | copy-done | bytes 917528
  5.2 0.0 copy-start.3
  5.3 1.0 %copy-done.3 = bf16[1,16,14336]{2,1,0:T(8,128)(2,1)S(1)} copy-done((bf16[1,16,14336]{2,1,0:T(8,128)(2,1)S(1)}, bf16[1,16,14336]{2,1,0:T(8,128)(2,1)}, u32[]{:S(2)}) %copy-start.3) | copy-done | bytes 458776
  6.3 0.0 copy-start.4
  6.3 0.7 copy-done.4
  7.0 0.0 copy-start.5
  7.0 0.7 copy-done.5
  7.6 0.0 copy-start.6
  7.6 0.7 copy-done.6
  8.3 0.0 copy-start.7
  8.3 0.7 copy-done.7
  8.9 79.6 %learned_update.1 = (bf16[1,128,14336]{2,1,0:T(8,128)(2,1)}, f32[1,16,14336]{2,1,0:T(8,128)S(1)}, f32[1,16,14336]{2,1,0:T(8,128)S(1)}) custom-call(s32[4,4]{1,0:T(4,128)S(1)} %copy-done.5, f32[6,32]{1,0:T(8,128)S(1)} %copy-done.4, f32[32]{0:T(128)S(1)} %copy-done.6, f32[32,2]{1,0:T(8,128)S(1)} %copy.12.out_weight, f32[2]{0:T(128)S(1)} %copy-done.7, ...), custom_call_target="tpu_custom_call" | custom-call | tf_op jit(solution)/shard_map/learned_update/pallas_call | solution.py:337
  88.6 4.2 %copy.16 = bf16[1,128,14336]{2,1,0:T(8,128)(2,1)} copy(bf16[1,128,14336]{2,1,0:T(8,128)(2,1)} %get-tuple-element.6) | data formatting | bytes 7340032
  92.8 0.9 copy.17
  93.7 0.9 copy.18
Async XLA Ops:
  1.4 1.5 %copy-start = (bf16[1,4,16,14336]{3,2,1,0:T(8,128)(2,1)S(1)}, bf16[1,4,16,14336]{3,2,1,0:T(8,128)(2,1)}, u32[]{:S(2)}) copy-start(bf16[1,4,16,14336]{3,2,1,0:T(8,128)(2,1)} %grads.1) | copy-start | bytes 5505028
  2.9 1.2 %copy-start.1 = (f32[1,16,14336]{2,1,0:T(8,128)S(1)}, f32[1,16,14336]{2,1,0:T(8,128)}, u32[]{:S(2)}) copy-start(f32[1,16,14336]{2,1,0:T(8,128)} %mom.1) | copy-start | bytes 2752516
  4.1 1.2 %copy-start.2 = (f32[1,16,14336]{2,1,0:T(8,128)S(1)}, f32[1,16,14336]{2,1,0:T(8,128)}, u32[]{:S(2)}) copy-start(f32[1,16,14336]{2,1,0:T(8,128)} %second.1) | copy-start | bytes 2752516
  5.2 1.0 %copy-start.3 = (bf16[1,16,14336]{2,1,0:T(8,128)(2,1)S(1)}, bf16[1,16,14336]{2,1,0:T(8,128)(2,1)}, u32[]{:S(2)}) copy-start(bf16[1,16,14336]{2,1,0:T(8,128)(2,1)} %weight.1) | copy-start | bytes 1376260
  6.3 0.7 copy-start.4
  7.0 0.7 copy-start.5
  7.6 0.7 copy-start.6
  8.3 0.7 copy-start.7

commit v2 on v1

v2 whole, which is shorter than its diff:
```python
import functools

import jax
import jax.numpy as jnp
from jax import lax
from jax.experimental import pallas as pl
from jax.experimental.pallas import tpu as pltpu
from jax.sharding import PartitionSpec as P

MOMENTUM_DECAY = 0.9
SECOND_DECAY = 0.99
NORM_EPS = 1e-06
ROOT_EPS = 1e-08
STEP_SCALE = 0.2
EXP_SCALE = 0.5
LANES = 128
MOST_CHUNKS = 14
MOST_CUTS = 4
LAG = 2
VMEM_BYTES = 67043328


def largest_divisor(number, most):
    return max(d for d in range(1, most + 1) if number % d == 0)


def tile_width(columns, most):
    return LANES * largest_divisor(columns // LANES, most // LANES)


def turned_chunks(depth, across, chunks):
    def load(turned):
        straight = chunks - turned
        on_x = (across - 1) * (depth * straight + turned)
        on_z = (depth - 1) * (straight + across * turned)
        return max(on_x, on_z)

    return min(range(chunks + 1), key=load)


def remote(src, dst, send_sem, recv_sem, axis, peer):
    return pltpu.make_async_remote_copy(
        src_ref=src,
        dst_ref=dst,
        send_sem=send_sem,
        recv_sem=recv_sem,
        device_id={axis: peer},
        device_id_type=pl.DeviceIdType.MESH,
    )


def kernel(
    groups,
    depth,
    across,
    chunks,
    counts_hbm,
    in_weight_hbm,
    in_bias_hbm,
    out_weight_hbm,
    out_bias_hbm,
    grads_hbm,
    weight_hbm,
    mom_hbm,
    second_hbm,
    gathered_hbm,
    mom_hbm_out,
    second_hbm_out,
    counts,
    in_weight,
    in_bias,
    out_weight,
    out_bias,
    grads,
    weight,
    mom,
    second,
    gathered,
    outgoing,
    arrived,
    gradient,
    sums,
    bias,
    small_sem,
    slab_sem,
    param_sem,
    grad_send,
    grad_recv,
    flush_sem,
    state_sem,
    sum_send,
    sum_recv,
    row_send,
    row_recv,
):
    shards = depth * across
    rows, columns = mom.shape
    units = in_bias.shape[0]
    me_group = lax.axis_index("ep")
    me = lax.axis_index("fs")
    z = me // across
    x = me % across

    def peer_of(step):
        return (me_group + step) % groups

    small = [
        pltpu.make_async_copy(src, dst, small_sem.at[i])
        for i, (src, dst) in enumerate(
            (
                (counts_hbm, counts),
                (in_weight_hbm, in_weight),
                (in_bias_hbm, in_bias),
                (out_weight_hbm, out_weight),
                (out_bias_hbm, out_bias),
            )
        )
    ]
    for copy in small:
        copy.start()

    slabs = [
        pltpu.make_async_copy(
            grads_hbm.at[0, peer_of(step)], grads.at[step], slab_sem.at[step]
        )
        for step in range(groups)
    ]
    for copy in slabs[1:] + slabs[:1]:
        copy.start()
    params = [
        pltpu.make_async_copy(src.at[0], dst, param_sem.at[i])
        for i, (src, dst) in enumerate(
            (
                (mom_hbm, mom),
                (second_hbm, second),
                (weight_hbm, weight),
            )
        )
    ]
    for copy in params:
        copy.start()

    barrier = pltpu.get_barrier_semaphore()
    for step in range(1, groups):
        pl.semaphore_signal(
            barrier,
            inc=1,
            device_id={"ep": peer_of(step)},
            device_id_type=pl.DeviceIdType.MESH,
        )
    for step in range(1, shards):
        pl.semaphore_signal(
            barrier,
            inc=1,
            device_id={"fs": (me + step) % shards},
            device_id_type=pl.DeviceIdType.MESH,
        )
    pl.semaphore_wait(barrier, groups - 1 + shards - 1)
    for copy in small:
        copy.wait()

    cuts = grad_recv.shape[1]
    cut = columns // cuts
    narrow = tile_width(cut, 512)

    def cols_of(c, i):
        return pl.ds(pl.multiple_of(c * cut + i * narrow, narrow), narrow)

    def piece_of(c):
        return pl.ds(pl.multiple_of(c * cut, cut), cut)

    def share_of(expert):
        total = counts[0, expert]
        for s in range(1, groups):
            total = total + counts[s, expert]
        mine = jnp.full((1, LANES), counts[me_group, expert].astype(jnp.float32))
        return (mine / jnp.full((1, LANES), total.astype(jnp.float32)))[:, :1]

    shares = [share_of(peer_of(step)) for step in range(groups)]

    def weighted(step, cols):
        value = shares[step] * grads[step, :, cols].astype(jnp.float32)
        return value.astype(jnp.bfloat16)

    def grad_copy(step, c):
        return remote(
            outgoing.at[step - 1, :, piece_of(c)],
            arrived.at[step - 1, :, piece_of(c)],
            grad_send.at[step - 1, c],
            grad_recv.at[step - 1, c],
            "ep",
            peer_of(step),
        )

    order = sorted(range(1, groups), key=lambda step: abs(2 * step - groups))
    for copy in slabs:
        copy.wait()

    def send_piece(c, carry):
        for step in order:

            def weigh(i, inner, step=step):
                cols = cols_of(c, i)
                outgoing[step - 1, :, cols] = weighted(step, cols)
                return inner

            lax.fori_loop(0, cut // narrow, weigh, 0)
            grad_copy(step, c).start()
        return carry

    lax.fori_loop(0, cuts, send_piece, 0)
    for copy in params:
        copy.wait()


    def moments(c, carry):
        for step in range(1, groups):
            grad_copy(step, c).wait_recv()

        def one(i, inner):
            grad_acc, mom_acc = inner
            cols = cols_of(c, i)
            total = weighted(0, cols).astype(jnp.float32)
            for step in range(1, groups):
                total = total + arrived[step - 1, :, cols].astype(jnp.float32)
            mom_next = MOMENTUM_DECAY * mom[:, cols] + (1.0 - MOMENTUM_DECAY) * total
            gradient[:, cols] = total
            mom[:, cols] = mom_next
            second[:, cols] = (
                SECOND_DECAY * second[:, cols] + (1.0 - SECOND_DECAY) * total * total
            )
            return grad_acc + total * total, mom_acc + mom_next * mom_next

        return lax.fori_loop(0, cut // narrow, one, carry)

    zero = jnp.zeros((rows, narrow), jnp.float32)
    grad_acc, mom_acc = lax.fori_loop(0, cuts, moments, (zero, zero))

    def to_lanes(acc):
        acc = jnp.sum(acc, axis=0, keepdims=True)
        return sum(acc[:, j : j + LANES] for j in range(0, narrow, LANES))

    sums[me, 0:1, :] = to_lanes(grad_acc)
    sums[me, 1:2, :] = to_lanes(mom_acc)
    sum_sends = []
    for step in range(1, shards):
        copy = remote(
            sums.at[me],
            sums.at[me],
            sum_send.at[step - 1],
            sum_recv.at[me],
            "fs",
            (me + step) % shards,
        )
        copy.start()
        sum_sends.append(copy)
    for step in range(1, shards):
        source = (me + step) % shards
        remote(
            sums.at[source],
            sums.at[source],
            sum_send.at[step - 1],
            sum_recv.at[source],
            "fs",
            source,
        ).wait_recv()

    states = [
        pltpu.make_async_copy(mom, mom_hbm_out.at[0], state_sem.at[0]),
        pltpu.make_async_copy(second, second_hbm_out.at[0], state_sem.at[1]),
    ]
    for copy in states:
        copy.start()

    entries = rows * columns * shards
    totals = sums[0]
    for s in range(1, shards):
        totals = totals + sums[s]
    mean = jnp.broadcast_to(jnp.sum(totals, axis=1, keepdims=True) / entries, (2, LANES)) + NORM_EPS
    inverse = lax.rsqrt(mean)
    inv_grad = inverse[0:1, :1]
    inv_mom = inverse[1:2, :1]
    log_mom = jnp.max(0.5 * jnp.log(mean[1:2, :]))
    for h in range(units):
        bias[h] = in_bias[h] + in_weight[5, h] * log_mom

    width = columns // chunks
    tile = tile_width(width, 256)

    def learned_step(cols):
        grad = gradient[:, cols]
        mom_next = mom[:, cols]
        old = weight[:, cols].astype(jnp.float32)
        inv_root = lax.rsqrt(second[:, cols] + ROOT_EPS)
        features = (
            grad * inv_grad,
            mom_next * inv_mom,
            mom_next * inv_root,
            grad * inv_root,
            old,
        )
        direction = jnp.full(grad.shape, out_bias[0])
        magnitude = jnp.full(grad.shape, out_bias[1])
        for h in range(units):
            hidden = features[0] * in_weight[0, h] + bias[h]
            for f in range(1, len(features)):
                hidden = hidden + features[f] * in_weight[f, h]
            hidden = jnp.maximum(hidden, 0.0)
            direction = direction + hidden * out_weight[0, h]
            magnitude = magnitude + hidden * out_weight[1, h]
        update = STEP_SCALE * direction * jnp.exp(EXP_SCALE * magnitude)
        return (old - update).astype(jnp.bfloat16)

    def rows_of(source):
        return pl.ds(pl.multiple_of(source * rows, rows), rows)

    ways = (
        (across, z < depth - 1),
        (-across, z > 0),
        (1, x < across - 1),
        (-1, x > 0),
    )
    turned = turned_chunks(depth, across, chunks)
    along_z = (z, depth, across, (0, 1))
    along_x = (x, across, 1, (2, 3))
    trees = ((along_x, along_z, 0, turned), (along_z, along_x, turned, chunks))

    def block(source, k):
        return gathered.at[rows_of(source), pl.ds(pl.multiple_of(k * width, width), width)]

    def send(tree, source, k, which):
        for number in which:
            offset, possible = ways[number]

            @pl.when(possible)
            def _(number=number, offset=offset):
                piece = block(source, k)
                remote(
                    piece,
                    piece,
                    row_send.at[tree, number, source],
                    row_recv.at[source, k],
                    "fs",
                    me + offset,
                ).start()

    def flush(source, k):
        cols = pl.ds(pl.multiple_of(k * width, width), width)
        pltpu.make_async_copy(
            block(source, k), gathered_hbm.at[0, rows_of(source), cols], flush_sem.at[source]
        ).start()

    def await_block(source, k):
        piece = block(source, k)
        remote(
            piece, piece, row_send.at[0, 0, source], row_recv.at[source, k], "fs", source
        ).wait_recv()

    def relay(t, tree):
        first, second, low, high = trees[tree]
        if low == high:
            return
        at, size, stride, (up, down) = first
        for d in range(1, size):
            k = t - LAG * d
            live = jnp.logical_and(k >= low, k < high)

            @pl.when(jnp.logical_and(live, at >= d))
            def _(d=d, k=k):
                source = me - d * stride
                await_block(source, k)
                send(tree, source, k, (up,) + second[3])
                flush(source, k)

            @pl.when(jnp.logical_and(live, at + d < size))
            def _(d=d, k=k):
                source = me + d * stride
                await_block(source, k)
                send(tree, source, k, (down,) + second[3])
                flush(source, k)

        other, length, pitch, (up_other, down_other) = second
        for e in range(1, length):
            k = t - LAG * (size - 1 + e)
            live = jnp.logical_and(k >= low, k < high)
            for level in range(size):

                @pl.when(jnp.logical_and(live, other >= e))
                def _(e=e, k=k, level=level):
                    source = level * stride + (other - e) * pitch
                    await_block(source, k)
                    send(tree, source, k, (up_other,))
                    flush(source, k)

                @pl.when(jnp.logical_and(live, other + e < length))
                def _(e=e, k=k, level=level):
                    source = level * stride + (other + e) * pitch
                    await_block(source, k)
                    send(tree, source, k, (down_other,))
                    flush(source, k)

    def turn(t, carry):
        @pl.when(t < chunks)
        def _():
            def one(i, inner):
                cols = pl.ds(pl.multiple_of(t * width + i * tile, tile), tile)
                gathered[rows_of(me), cols] = learned_step(cols)
                return inner

            lax.fori_loop(0, width // tile, one, 0)

        for tree in range(2):
            _, _, low, high = trees[tree]

            @pl.when(jnp.logical_and(t >= low, t < high))
            def _(tree=tree):
                send(tree, me, t, (0, 1, 2, 3))
                flush(me, t)

        for tree in range(2):
            relay(t, tree)
        return carry

    lax.fori_loop(0, chunks + LAG * (depth - 1 + across - 1), turn, 0)

    def drain(c, carry):
        for step in range(1, groups):
            grad_copy(step, c).wait_send()
        return carry

    lax.fori_loop(0, cuts, drain, 0)
    for copy in sum_sends:
        copy.wait_send()
    for copy in states:
        copy.wait()
    for source in range(shards):
        pltpu.make_async_copy(
            gathered.at[rows_of(source), :],
            gathered_hbm.at[0, rows_of(source), :],
            flush_sem.at[source],
        ).wait()
    for tree in range(2):
        first, _, low, high = trees[tree]
        if low == high:
            continue
        for number, (_, possible) in enumerate(ways):
            for source in range(shards):
                level, place = source // across, source % across
                used = (level <= z, level >= z, place <= x, place >= x)[number]
                if first is along_z and number < 2:
                    used = jnp.logical_and(used, place == x)
                if first is along_x and number >= 2:
                    used = jnp.logical_and(used, level == z)

                @pl.when(jnp.logical_and(possible, used))
                def _(tree=tree, number=number, source=source, low=low, high=high):
                    piece = gathered.at[rows_of(source), pl.ds(low * width, (high - low) * width)]
                    remote(
                        piece,
                        piece,
                        row_send.at[tree, number, source],
                        row_recv.at[source, low],
                        "fs",
                        (me + 1) % shards,
                    ).wait_send()


def per_device(
    groups, shards, grads, counts, weight, mom, second, in_weight, in_bias, out_weight, out_bias
):
    rows, columns = mom.shape[1], mom.shape[2]
    across = max(d for d in range(1, shards + 1) if shards % d == 0 and d * d <= shards)
    depth = shards // across
    chunks = largest_divisor(columns // LANES, MOST_CHUNKS)
    cuts = largest_divisor(columns // LANES, MOST_CUTS)
    hbm = pl.BlockSpec(memory_space=pltpu.HBM)
    return pl.pallas_call(
        functools.partial(kernel, groups, depth, across, chunks),
        out_shape=(
            jax.ShapeDtypeStruct((1, rows * shards, columns), jnp.bfloat16),
            jax.ShapeDtypeStruct(mom.shape, jnp.float32),
            jax.ShapeDtypeStruct(second.shape, jnp.float32),
        ),
        in_specs=[hbm] * 9,
        out_specs=(hbm, hbm, hbm),
        scratch_shapes=[
            pltpu.SMEM(counts.shape, jnp.int32),
            pltpu.SMEM(in_weight.shape, jnp.float32),
            pltpu.SMEM(in_bias.shape, jnp.float32),
            pltpu.SMEM(out_weight.shape[::-1], jnp.float32),
            pltpu.SMEM(out_bias.shape, jnp.float32),
            pltpu.VMEM((groups, rows, columns), jnp.bfloat16),
            pltpu.VMEM((rows, columns), jnp.bfloat16),
            pltpu.VMEM((rows, columns), jnp.float32),
            pltpu.VMEM((rows, columns), jnp.float32),
            pltpu.VMEM((rows * shards, columns), jnp.bfloat16),
            pltpu.VMEM((groups - 1, rows, columns), jnp.bfloat16),
            pltpu.VMEM((groups - 1, rows, columns), jnp.bfloat16),
            pltpu.VMEM((rows, columns), jnp.float32),
            pltpu.VMEM((shards, 2, LANES), jnp.float32),
            pltpu.SMEM((in_bias.shape[0],), jnp.float32),
            pltpu.SemaphoreType.DMA((5,)),
            pltpu.SemaphoreType.DMA((groups,)),
            pltpu.SemaphoreType.DMA((3,)),
            pltpu.SemaphoreType.DMA((groups - 1, cuts)),
            pltpu.SemaphoreType.DMA((groups - 1, cuts)),
            pltpu.SemaphoreType.DMA((shards,)),
            pltpu.SemaphoreType.DMA((2,)),
            pltpu.SemaphoreType.DMA((shards - 1,)),
            pltpu.SemaphoreType.DMA((shards,)),
            pltpu.SemaphoreType.DMA((2, 4, shards)),
            pltpu.SemaphoreType.DMA((shards, chunks)),
        ],
        compiler_params=pltpu.CompilerParams(
            collective_id=0, has_side_effects=True, vmem_limit_bytes=VMEM_BYTES
        ),
        name="learned_update",
    )(counts, in_weight, in_bias, out_weight.T, out_bias, grads, weight, mom, second)


def solution(mesh):
    in_specs = (
        P("ep", None, "fs", None),
        P(),
        P("ep", "fs", None),
        P("ep", "fs", None),
        P("ep", "fs", None),
        P(),
        P(),
        P(),
        P(),
    )
    out_specs = (P("ep", None, None), P("ep", "fs", None), P("ep", "fs", None))
    body = functools.partial(per_device, mesh.shape["ep"], mesh.shape["fs"])
    return jax.shard_map(
        body, mesh=mesh, in_specs=in_specs, out_specs=out_specs, check_vma=False
    )
```

time: 95 us -> 86.5 us (0.911)
  local copies, waits for them, and re-layouts: 14.4 us -> 6.18 us
    unnamed x20 -> x7, local copies, waits for them, and re-layouts: 14.4 us -> 6.18 us
where the time goes in v2:
time: 86.5 us; the launch traced here: 86.3 us
  Pallas kernels  79.5 us (92%)
  local copies, waits for them, and re-layouts  6.18 us (7%)
    pallas_call x1, Pallas kernels, per_device(): pl.pallas_call(functools.partial(kernel, groups, depth, across, chunks),...  79.5 us
    unnamed x7, local copies, waits for them, and re-layouts  6.18 us

profile of v2, /device:TPU:0, one launch (start us, length us, event | category | flops | bytes accessed | tf_op | source)
XLA Modules:
  0.0 86.3 jit_solution(14828402430493107429)
XLA Ops:
  0.6 79.5 %learned_update.1 = (bf16[1,128,14336]{2,1,0:T(8,128)(2,1)}, f32[1,16,14336]{2,1,0:T(8,128)}, f32[1,16,14336]{2,1,0:T(8,128)}) custom-call(s32[4,4]{1,0:T(4,128)} %counts_hbm.1, f32[6,32]{1,0:T(8,128)} %in_weight_hbm.1, f32[32]{0:T(128)} %in_bias_hbm.1, f32[2,32]{1,0:T(2,128)} %bitcast.1, f32[2]{0:T(128)} %out_bias_hbm.1, ...), custom_call_target="tpu_custom_call" | custom-call | tf_op jit(solution)/shard_map/learned_update/pallas_call | solution.py:477
  80.1 0.0 copy-start.1
  80.1 0.0 copy-start
  80.1 4.3 %copy.15 = bf16[1,128,14336]{2,1,0:T(8,128)(2,1)} copy(bf16[1,128,14336]{2,1,0:T(8,128)(2,1)} %get-tuple-element.6) | data formatting | bytes 7340032
  84.5 0.0 copy-done.1
  84.5 0.9 %copy.16 = f32[1,16,14336]{2,1,0:T(8,128)} copy(f32[1,16,14336]{2,1,0:T(8,128)S(1)} %copy-done.1) | data formatting | bytes 1835008
  85.4 0.0 copy-done
  85.4 0.9 %copy.17 = f32[1,16,14336]{2,1,0:T(8,128)} copy(f32[1,16,14336]{2,1,0:T(8,128)S(1)} %copy-done) | data formatting | bytes 1835008
Async XLA Ops:
  80.1 4.4 %copy-start.1 = (f32[1,16,14336]{2,1,0:T(8,128)S(1)}, f32[1,16,14336]{2,1,0:T(8,128)}, u32[]{:S(2)}) copy-start(f32[1,16,14336]{2,1,0:T(8,128)} %get-tuple-element.7) | copy-start | bytes 2752516
  80.1 5.3 %copy-start = (f32[1,16,14336]{2,1,0:T(8,128)S(1)}, f32[1,16,14336]{2,1,0:T(8,128)}, u32[]{:S(2)}) copy-start(f32[1,16,14336]{2,1,0:T(8,128)} %get-tuple-element.8) | copy-start | bytes 2752516

commit v3 on v2

--- a/solution.py
+++ b/solution.py
@@ -16,7 +16,7 @@
 LANES = 128
 MOST_CHUNKS = 14
 MOST_CUTS = 4
-LAG = 2
+LAG = 3
 VMEM_BYTES = 67043328
 
 

time: 86.5 us -> 83.4 us (0.964)
  Pallas kernels: 79.5 us -> 76.4 us
    pallas_call x1, Pallas kernels: 79.5 us -> 76.4 us  [per_device(): pl.pallas_call(functools.partial(kernel, groups, depth, across, chunks),...]
where the time goes in v3:
time: 83.4 us; the launch traced here: 83.2 us
  Pallas kernels  76.4 us (92%)
  local copies, waits for them, and re-layouts  6.18 us (7%)
    pallas_call x1, Pallas kernels, per_device(): pl.pallas_call(functools.partial(kernel, groups, depth, across, chunks),...  76.4 us
    unnamed x7, local copies, waits for them, and re-layouts  6.18 us

profile of v3, /device:TPU:0, one launch (start us, length us, event | category | flops | bytes accessed | tf_op | source)
XLA Modules:
  0.0 83.2 jit_solution(16970597023861139422)
XLA Ops:
  0.6 76.4 %learned_update.1 = (bf16[1,128,14336]{2,1,0:T(8,128)(2,1)}, f32[1,16,14336]{2,1,0:T(8,128)}, f32[1,16,14336]{2,1,0:T(8,128)}) custom-call(s32[4,4]{1,0:T(4,128)} %counts_hbm.1, f32[6,32]{1,0:T(8,128)} %in_weight_hbm.1, f32[32]{0:T(128)} %in_bias_hbm.1, f32[2,32]{1,0:T(2,128)} %bitcast.1, f32[2]{0:T(128)} %out_bias_hbm.1, ...), custom_call_target="tpu_custom_call" | custom-call | tf_op jit(solution)/shard_map/learned_update/pallas_call | solution.py:477
  77.0 0.0 copy-start.1
  77.1 0.0 copy-start
  77.1 4.3 %copy.15 = bf16[1,128,14336]{2,1,0:T(8,128)(2,1)} copy(bf16[1,128,14336]{2,1,0:T(8,128)(2,1)} %get-tuple-element.6) | data formatting | bytes 7340032
  81.4 0.0 copy-done.1
  81.4 0.9 %copy.16 = f32[1,16,14336]{2,1,0:T(8,128)} copy(f32[1,16,14336]{2,1,0:T(8,128)S(1)} %copy-done.1) | data formatting | bytes 1835008
  82.3 0.0 copy-done
  82.3 0.9 %copy.17 = f32[1,16,14336]{2,1,0:T(8,128)} copy(f32[1,16,14336]{2,1,0:T(8,128)S(1)} %copy-done) | data formatting | bytes 1835008
Async XLA Ops:
  77.0 4.4 %copy-start.1 = (f32[1,16,14336]{2,1,0:T(8,128)S(1)}, f32[1,16,14336]{2,1,0:T(8,128)}, u32[]{:S(2)}) copy-start(f32[1,16,14336]{2,1,0:T(8,128)} %get-tuple-element.7) | copy-start | bytes 2752516
  77.1 5.3 %copy-start = (f32[1,16,14336]{2,1,0:T(8,128)S(1)}, f32[1,16,14336]{2,1,0:T(8,128)}, u32[]{:S(2)}) copy-start(f32[1,16,14336]{2,1,0:T(8,128)} %get-tuple-element.8) | copy-start | bytes 2752516
